TPU v7x, 32 devices: a whole 2x2x4 slice. The times are simulated.
32 devices in a mesh: ens: 2 (over y), space: 4 (over z), tm: 2 (over x), mom: 2 (over core).
Axes of the slice: x: 2, y: 2, z: 4, core: 2. Of those that a mesh axis runs over, the one named last changes fastest.
Arguments:
- eigvecs: bfloat16 [8, 2, 3, 256, 2048], P(('ens', 'tm'), None, None, None, 'space'), parts along dimension 0, may hold values from -0.359375 to 0.359375
- momenta: int32 [4, 3], P('mom'), may hold values from 1 to 2
- pairs: int32 [2, 2], replicated, may hold values from 0 to 3, as said below
- spin_weights: float32 [4, 4], replicated, may hold values from -1 to 1
- perambulators: bfloat16 [4, 2, 4, 4, 256, 256], P(('ens', 'tm'), None, None, None, 'space'), parts along dimension 0, may hold values from -0.0234375 to 0.0234375
Outputs:
- blocks: bfloat16 [4, 4, 2, 256, 256], P(('ens', 'tm'), 'mom', None, 'space'), parts along dimension 0
There are 2 independent parts, one for each index of `ens`. A program takes and returns all parts, laid end to end along the dimension named above; an argument that names none is the same for every part. Nothing has to cross between parts.
Inputs may be any that keep to these rules, and one draw needn't show every extreme that they name: pairs[q, 0], the sink, lies in time group q: (q) * 2 <= pairs[q, 0] < (q + 1) * 2; pairs[q, 1], the source, is any timeslice.
All inputs are finite; a program needn't handle non-finite values.
Results may differ from a plain program's by a relative error of at most 0.008.
Values may be sent and summed in bfloat16 or wider, within the bound.
A program may use at most 64 MiB of HBM per device.

v0:
```python
import math

import jax
import jax.numpy as jnp
from jax import lax
from jax.sharding import PartitionSpec as P

LAT = 48


EXACT_PRECISION = lax.Precision.HIGHEST


def phases(momenta, site_ids):
    xcoord = (site_ids % LAT).astype(jnp.float32)
    ycoord = (site_ids // LAT % LAT).astype(jnp.float32)
    zcoord = (site_ids // (LAT * LAT)).astype(jnp.float32)
    mom_float = momenta.astype(jnp.float32)
    angles = (
        mom_float[:, 0:1] * xcoord + mom_float[:, 1:2] * ycoord + mom_float[:, 2:3] * zcoord
    ) * (2.0 * math.pi / LAT)
    return (jnp.cos(angles), jnp.sin(angles))


def elemental_terms(eigvecs, cosine_rows, sine_rows):
    contract_dims = (((0, 2), (0, 2)), ((), ()))
    per_time = []
    for which_time in range(eigvecs.shape[0]):
        real_vec = eigvecs[which_time, 0]
        imag_vec = eigvecs[which_time, 1]
        real_wide = real_vec.astype(jnp.float32)
        imag_wide = imag_vec.astype(jnp.float32)
        per_mom = []
        for which_mom in range(cosine_rows.shape[0]):
            cosine = cosine_rows[which_mom]
            sine = sine_rows[which_mom]
            real_turned = (cosine * real_wide + sine * imag_wide).astype(jnp.bfloat16)
            imag_turned = (cosine * imag_wide - sine * real_wide).astype(jnp.bfloat16)
            real_part = lax.dot_general(
                real_vec, real_turned, contract_dims, preferred_element_type=jnp.float32
            ) + lax.dot_general(
                imag_vec, imag_turned, contract_dims, preferred_element_type=jnp.float32
            )
            imag_part = lax.dot_general(
                real_vec, imag_turned, contract_dims, preferred_element_type=jnp.float32
            ) - lax.dot_general(
                imag_vec, real_turned, contract_dims, preferred_element_type=jnp.float32
            )
            per_mom.append(jnp.stack([real_part, imag_part]))
        per_time.append(jnp.stack(per_mom))
    return jnp.stack(per_time)


def source_slots(held_rows, pairs, my_group, times_dev, tm_size, pair_dev):
    wanted = pairs[:, 1].reshape(tm_size, pair_dev)
    local_times = jnp.arange(times_dev, dtype=jnp.int32) + my_group * times_dev
    chosen = (wanted[:, :, None] == local_times).astype(jnp.bfloat16)
    return jnp.einsum(
        "rqt,tmcij->rqmcij", chosen, held_rows, preferred_element_type=jnp.float32
    ).astype(jnp.bfloat16)


def sink_select(held_rows, my_pairs, my_group, times_dev):
    local_times = jnp.arange(times_dev, dtype=jnp.int32) + my_group * times_dev
    chosen = (my_pairs[:, 0][:, None] == local_times).astype(jnp.bfloat16)
    return jnp.einsum(
        "qt,tmcij->qmcij", chosen, held_rows, preferred_element_type=jnp.float32
    ).astype(jnp.bfloat16)


def bridge(mixed_block, source):
    real_part = jnp.einsum(
        "qkl,qmjl->qmkj", mixed_block[:, 0], source[:, :, 0], preferred_element_type=jnp.float32
    ) + jnp.einsum(
        "qkl,qmjl->qmkj", mixed_block[:, 1], source[:, :, 1], preferred_element_type=jnp.float32
    )
    imag_part = jnp.einsum(
        "qkl,qmjl->qmkj", mixed_block[:, 1], source[:, :, 0], preferred_element_type=jnp.float32
    ) - jnp.einsum(
        "qkl,qmjl->qmkj", mixed_block[:, 0], source[:, :, 1], preferred_element_type=jnp.float32
    )
    return jnp.stack([real_part, imag_part], 2).astype(jnp.bfloat16)


def attach(sink_elem, bridged):
    real_part = jnp.einsum(
        "qmik,qmkj->qmij", sink_elem[:, :, 0], bridged[:, :, 0], preferred_element_type=jnp.float32
    ) - jnp.einsum(
        "qmik,qmkj->qmij", sink_elem[:, :, 1], bridged[:, :, 1], preferred_element_type=jnp.float32
    )
    imag_part = jnp.einsum(
        "qmik,qmkj->qmij", sink_elem[:, :, 0], bridged[:, :, 1], preferred_element_type=jnp.float32
    ) + jnp.einsum(
        "qmik,qmkj->qmij", sink_elem[:, :, 1], bridged[:, :, 0], preferred_element_type=jnp.float32
    )
    return jnp.stack([real_part, imag_part], 2)


def local(eigvecs, momenta, pairs, spin_weights, perambulators):
    times_dev = eigvecs.shape[0]
    vec_count = eigvecs.shape[3]
    sites_dev = eigvecs.shape[4]
    pair_dev = perambulators.shape[0]
    tm_size = lax.axis_size("tm")
    space_size = lax.axis_size("space")
    my_group = lax.axis_index("tm")
    my_place = lax.axis_index("space")
    rows_dev = vec_count // space_size
    row_first = my_place * rows_dev
    site_ids = my_place * sites_dev + jnp.arange(sites_dev, dtype=jnp.int32)
    cosine_rows, sine_rows = phases(momenta, site_ids)
    partial_value = elemental_terms(eigvecs, cosine_rows, sine_rows)
    my_pairs = lax.dynamic_slice_in_dim(pairs, my_group * pair_dev, pair_dev, 0)
    whole = lax.psum(partial_value, "space").astype(jnp.bfloat16)
    outgoing = source_slots(whole, pairs, my_group, times_dev, tm_size, pair_dev)
    arrived = lax.all_to_all(outgoing, "tm", split_axis=0, concat_axis=0, tiled=True)
    source_full = jnp.sum(arrived, axis=0, dtype=jnp.float32).astype(jnp.bfloat16)
    sink_whole = sink_select(whole, my_pairs, my_group, times_dev)
    sink_own = lax.dynamic_slice_in_dim(sink_whole, row_first, rows_dev, 3)
    mixed_peramb = jnp.einsum(
        "ab,qcabkl->qckl",
        spin_weights,
        perambulators.astype(jnp.float32),
        precision=EXACT_PRECISION,
    ).astype(jnp.bfloat16)
    bridged = bridge(lax.all_gather(mixed_peramb, "space", axis=2, tiled=True), source_full)
    blocks = attach(sink_own, bridged).astype(jnp.bfloat16)
    return blocks


def solution(mesh):
    return jax.shard_map(
        local,
        mesh=mesh,
        in_specs=(
            P(("ens", "tm"), None, None, None, "space"),
            P("mom", None),
            P(),
            P(),
            P(("ens", "tm"), None, None, None, "space", None),
        ),
        out_specs=P(("ens", "tm"), "mom", None, "space", None),
        check_vma=False,
    )
```

profile of v0, /device:TPU:0, one launch (start us, length us, event | category | flops | bytes accessed | tf_op | source)
XLA Modules:
  0.0 120.1 jit_solution(8111220607492806430)
XLA Ops:
  0.0 0.0 copy-start
  0.0 0.8 convert_element_type.166
  0.8 0.2 slice_reduce_fusion.3
  1.0 0.1 fusion.149
  1.1 0.1 sin.3
  1.3 0.0 copy-start.1
  1.3 2.2 %convolution_bitcast_fusion.14 = f32[256,256]{1,0:T(8,128)S(1)} fusion(f32[512]{0:T(512)S(1)} %bitcast.288, f32[512]{0:T(512)S(1)} %bitcast.296, bf16[2,2,3,256,512]{4,3,2,1,0:T(8,128)(2,1)} %param.5), kind=kOutput, calls=%fused_computation.55 | convolution fusion | flops 203685888 | bytes 2625536 | tf_op jit(solution)/shard_map/dot_general | solution.py:41
  3.5 0.4 copy-done.1
  3.9 0.4 convolution_bitcast_fusion.12
  4.3 0.5 convolution_bitcast_fusion.10
  4.8 0.4 convolution_bitcast_fusion.8
  5.2 0.4 convolution_bitcast_fusion.6
  5.7 0.5 convolution_bitcast_fusion.4
  6.1 0.5 convolution_bitcast_fusion.2
  6.6 0.4 convolution_bitcast_fusion
  7.1 0.4 fusion.22
  7.5 0.5 fusion.24
  8.0 0.5 fusion.26
  8.4 0.5 fusion.28
  8.9 0.5 fusion.30
  9.4 0.5 fusion.32
  9.8 0.5 fusion.34
  10.3 0.5 fusion.36
  10.8 0.1 maximum_bitcast_fusion
  11.0 0.1 maximum_bitcast_fusion.1
  11.1 0.1 pad_maximum_fusion
  11.2 79.3 %all-reduce.1 = bf16[2,2,2,256,256]{3,4,2,1,0:T(8,128)(2,1)} all-reduce(f32[2,2,2,256,256]{3,4,2,1,0:T(8,128)S(1)} %pad_maximum_fusion), channel_id=1, replica_groups=mesh['ens'=2,'space'=4,'tm'=2,'mom'=2] {'space'}, use_global_device_ids=true, to_apply=%region_0.1 | all-reduce | flops 524288 | bytes 3145728 | tf_op jit(solution)/shard_map/psum | solution.py:114
  90.5 2.5 %copy.12 = bf16[2,2,2,256,256]{4,0,3,2,1:T(2,128)(2,1)S(1)} copy(bf16[2,2,2,256,256]{3,4,2,1,0:T(8,128)(2,1)} %all-reduce.1) | data formatting | bytes 2097152 | tf_op jit(solution)/shard_map/convert_element_type | solution.py:114
  93.1 0.0 copy-done.3
  93.1 0.2 slice_reduce_fusion
  93.3 1.3 %fusion.16 = bf16[2,1,2,2,256,256]{5,0,4,3,2,1:T(2,128)(2,1)S(1)} fusion(bf16[2,2,2,256,256]{4,0,3,2,1:T(2,128)(2,1)S(1)} %copy.12, s32[2]{0:T(128)S(1)} %iota_add_fusion.1, s32[2]{0:T(128)S(1)} %slice_reduce_fusion), kind=kOutput, calls=%fused_computation.34 | convolution fusion | flops 2621444 | bytes 2097168 | tf_op jit(solution)/shard_map/rqt,tmcij->rqmcij/dot_general | solution.py:58
  94.6 1.1 copy.13
  95.7 3.9 %all-to-all-start = ((bf16[2,1,2,2,256,256]{5,4,3,2,1,0:T(8,128)(2,1)}), bf16[2,1,2,2,256,256]{5,4,3,2,1,0:T(8,128)(2,1)S(1)}, u32[]{:S(2)}, u32[]{:S(2)}) async-start(bf16[2,1,2,2,256,256]{5,4,3,2,1,0:T(8,128)(2,1)} %copy.13), calls=%async_computation | async-start | bytes 2097152 | tf_op jit(solution)/shard_map/all_to_all | solution.py:116
  99.6 2.1 %fusion.41 = bf16[1,2,64,256,1]{3,0,4,2,1:T(2,128)(2,1)S(1)} fusion(f32[4,4,1,1,1]{1,2,0,4,3:T(1,128)S(1)} %bitcast.304, bf16[2,4,4,64,256]{4,3,2,1,0:T(8,128)(2,1)S(1)} %bitcast.261), kind=kOutput, calls=%fused_computation.82 | convolution fusion | flops 6291456 | bytes 1114176 | tf_op jit(solution)/shard_map/ab,qcabkl->qckl/dot_general | solution.py:120
  101.8 1.3 %fusion.145 = bf16[1,2,2,256,256]{4,0,3,2,1:T(2,128)(2,1)S(1)} fusion(bf16[2,2,2,256,256]{4,0,3,2,1:T(2,128)(2,1)S(1)} %copy.12, s32[]{:T(128)S(1)} %bitcast.305, s32[]{:T(128)S(6)} %mul.205), kind=kOutput, calls=%fused_computation.194 | convolution fusion | flops 1048580 | bytes 1572872 | tf_op jit(solution)/shard_map/qt,tmcij->qmcij/dot_general | solution.py:66
  103.0 0.1 copy.37
  103.1 13.8 %all-gather = bf16[2,256,256]{2,1,0:T(8,128)(2,1)S(1)} all-gather(bf16[2,64,256]{2,1,0:T(8,128)(2,1)S(1)} %bitcast.271), channel_id=2, replica_groups=mesh['ens'=2,'space'=4,'tm'=2,'mom'=2] {'space'}, dimensions={1}, use_global_device_ids=true | all-gather | bytes 327680 | tf_op jit(solution)/shard_map/all_gather | solution.py:126
  116.9 0.0 all-to-all-done
  116.9 0.5 reduce_sum.14
  117.5 0.2 fusion.100
  117.7 0.3 fusion.99
  118.0 0.3 fusion.20
  118.3 0.3 fusion.19
  118.5 0.2 fusion.135
  118.7 0.2 fusion.134
  118.9 0.2 fusion.40
  119.2 0.2 fusion.39
  119.4 0.7 copy.20
  (18 shorter events, 0.3 us)
Async XLA Ops:
  0.0 99.6 %copy-start = (bf16[1,2,4,4,64,256]{5,4,3,2,1,0:T(8,128)(2,1)S(1)}, bf16[1,2,4,4,64,256]{5,4,3,2,1,0:T(8,128)(2,1)}, u32[]{:S(2)}) copy-start(bf16[1,2,4,4,64,256]{5,4,3,2,1,0:T(8,128)(2,1)} %param.9) | copy-start | bytes 3145732
  1.3 2.6 %copy-start.1 = (bf16[2,2,3,256,512]{4,3,2,1,0:T(8,128)(2,1)S(1)}, bf16[2,2,3,256,512]{4,3,2,1,0:T(8,128)(2,1)}, u32[]{:S(2)}) copy-start(bf16[2,2,3,256,512]{4,3,2,1,0:T(8,128)(2,1)} %param.5) | copy-start | bytes 9437188
  90.5 2.6 %copy-start.3 = (s32[2,2]{1,0:T(2,128)S(1)}, s32[2,2]{1,0:T(2,128)}, u32[]{:S(2)}) copy-start(s32[2,2]{1,0:T(2,128)} %param.7) | copy-start | bytes 52
  95.7 3.9 %copy-start.2 = (f32[4,4]{1,0:T(4,128)S(1)}, f32[4,4]{1,0:T(4,128)}, u32[]{:S(2)}) copy-start(f32[4,4]{1,0:T(4,128)} %param.8) | copy-start | bytes 196
  95.7 21.2 %all-to-all-start = ((bf16[2,1,2,2,256,256]{5,4,3,2,1,0:T(8,128)(2,1)}), bf16[2,1,2,2,256,256]{5,4,3,2,1,0:T(8,128)(2,1)S(1)}, u32[]{:S(2)}, u32[]{:S(2)}) async-start(bf16[2,1,2,2,256,256]{5,4,3,2,1,0:T(8,128)(2,1)} %copy.13), calls=%async_computation | async-start | bytes 2097152 | tf_op jit(solution)/shard_map/all_to_all | solution.py:116
where the time goes:
time: 120 us
  blocking collectives  93.1 us (78%)
  matrix products  15.5 us (13%)
  local copies, waits for them, and re-layouts  5.32 us (4%)
  starting transfers between devices  3.89 us (3%)
  other arithmetic  1.86 us (2%)
    psum x1, blocking collectives, local(): whole = lax.psum(partial_value, 'space').astype(jnp.bfloat16)  79.3 us
    all_gather x1, blocking collectives, local(): lax.all_gather(mixed_peramb, 'space', axis=2, tiled=True)  13.8 us
    all_to_all x1, starting transfers between devices, local(): lax.all_to_all(outgoing, 'tm', split_axis=0, concat_axis=0, tiled=True)  3.89 us
    dot_general x4, matrix products, elemental_terms(): lax.dot_general(imag_vec, imag_turned, contract_dims, preferred_element_t...  3.57 us
    convert_element_type x1, local copies, waits for them, and re-layouts, local(): whole = lax.psum(partial_value, 'space').astype(jnp.bfloat16)  2.54 us
  transfers between devices with their start and end apart: 1, of which 0 were waited for; matrix products, arithmetic and copies ran while one was open for 3% of the time, Pallas kernels for 0%

commit v1 on v0

v1 whole, which is shorter than its diff:
```python
import functools
import math

import jax
import jax.numpy as jnp
from jax import lax
from jax.experimental import pallas as pl
from jax.experimental.pallas import tpu as pltpu
from jax.sharding import PartitionSpec as P

LAT = 48
MESH = pl.DeviceIdType.MESH
F32 = jnp.float32
BF16 = jnp.bfloat16
NT = (((1,), (1,)), ((), ()))
ROW_BLOCK = 32


def nt_dot(left, right):
    return lax.dot_general(left, right, NT, preferred_element_type=F32)


def nn_dot(left, right):
    return jnp.dot(left, right, preferred_element_type=F32)


def flat_rows(chunks):
    count, rows, cols = chunks.shape
    if rows % 16:
        return chunks.astype(F32).reshape(count * rows, cols).astype(chunks.dtype)
    return chunks.reshape(count * rows, cols)


def pick(index, values):
    chosen = values[0]
    for which in range(1, len(values)):
        chosen = jnp.where(index == which, values[which], chosen)
    return chosen


def kernel(
    dims, pairs_ref, spin_ref, mom_ref, eig_ref, per_ref, out_ref,
    vecs, turned, trig, per_buf, part, right_out, right_in, left_out, left_in,
    reduced, swap_out, swap_in, source, mixed,
    eig_sem, per_sem, rs_send, rs_recv, swap_send, swap_recv, ag_send, ag_recv,
    mix_send, mix_recv, core_send, core_recv,
):
    (space, groups, times, moms, colours, vec_count, sites, pair_dev, spin) = dims
    rows = vec_count // space
    half = space // 2
    width = colours * sites
    me = lax.axis_index("space")
    group = lax.axis_index("tm")
    core = lax.axis_index("mom")
    right = lax.rem(me + 1, space)
    left = lax.rem(me + space - 1, space)
    other_core = 1 - core
    sent = []

    barrier = pltpu.get_barrier_semaphore()
    friends = [{"space": lax.rem(me + step, space)} for step in range(1, space)]
    friends += [{"tm": lax.rem(group + step, groups)} for step in range(1, groups)]
    friends += [{"mom": other_core}]
    for friend in friends:
        pl.semaphore_signal(barrier, inc=1, device_id=friend, device_id_type=MESH)

    def remote(src, dst, send_sem, recv_sem, target):
        return pltpu.make_async_remote_copy(
            src_ref=src, dst_ref=dst, send_sem=send_sem, recv_sem=recv_sem,
            device_id=target, device_id_type=MESH,
        )

    def launch(copy):
        copy.start()
        sent.append(copy)

    per_copy = pltpu.make_async_copy(per_ref.at[:, core], per_buf, per_sem)
    per_copy.start()
    eig_copies = []
    for t in range(times):
        of_time = []
        for c in range(2):
            for colour in range(colours):
                first = (c * colours + colour) * sites
                copy = pltpu.make_async_copy(
                    eig_ref.at[t, c, colour], vecs.at[t, :, pl.ds(first, sites)],
                    eig_sem.at[t, c, colour],
                )
                copy.start()
                of_time.append(copy)
        eig_copies.append(of_time)

    site = (lax.broadcasted_iota(jnp.int32, (8, sites), 1) + me * sites).astype(F32)
    line = jnp.floor((site + 0.5) * (1.0 / LAT))
    xcoord = site - line * LAT
    zcoord = jnp.floor((line + 0.5) * (1.0 / LAT))
    ycoord = line - zcoord * LAT
    for m in range(moms):
        turns = (
            mom_ref[m, 0].astype(F32) * xcoord
            + mom_ref[m, 1].astype(F32) * ycoord
            + mom_ref[m, 2].astype(F32) * zcoord
        )
        angle = turns * (2.0 * math.pi / LAT)
        trig[m, 0] = jnp.cos(angle)
        trig[m, 1] = jnp.sin(angle)

    per_copy.wait()
    for q in range(pair_dev):
        total = jnp.zeros((rows, vec_count), F32)
        for a in range(spin):
            for b in range(spin):
                total = total + spin_ref[a, b] * per_buf[q, a, b].astype(F32)
        mixed[me, core, q] = total.astype(BF16)

    pl.semaphore_wait(barrier, len(friends))

    def mix_hop(step, owner):
        return remote(
            mixed.at[owner, core], mixed.at[owner, core], mix_send.at[step - 1],
            mix_recv.at[step - 1], {"space": lax.rem(me + step, space)},
        )

    def core_hop(step):
        owner = lax.rem(me + space - step, space)
        return remote(
            mixed.at[owner, core], mixed.at[owner, core], core_send.at[step],
            core_recv.at[step], {"mom": other_core},
        )

    for step in range(1, space):
        launch(mix_hop(step, me))
    launch(core_hop(0))

    def build(unit, m, t):
        if m == 0:
            for copy in eig_copies[t]:
                copy.wait()
        cosine = trig[m, 0][None]
        sine = trig[m, 1][None]

        def block(step, carry):
            first = pl.multiple_of(step * ROW_BLOCK, ROW_BLOCK)
            span = pl.ds(first, ROW_BLOCK)
            for colour in range(colours):
                real_at = pl.ds(colour * sites, sites)
                imag_at = pl.ds((colours + colour) * sites, sites)
                shape = (ROW_BLOCK // 8, 8, sites)
                real = vecs[t, span, real_at].astype(F32).reshape(shape)
                imag = vecs[t, span, imag_at].astype(F32).reshape(shape)
                turned[span, real_at] = (
                    (cosine * real + sine * imag).reshape(ROW_BLOCK, sites).astype(BF16)
                )
                turned[span, imag_at] = (
                    (cosine * imag - sine * real).reshape(ROW_BLOCK, sites).astype(BF16)
                )
            return carry

        lax.fori_loop(0, vec_count // ROW_BLOCK, block, 0)
        real_part = nt_dot(vecs[t], turned[...])
        imag_part = nt_dot(vecs[t, :, :width], turned[:, width:]) - nt_dot(
            vecs[t, :, width:], turned[:, :width]
        )
        part[unit, 0] = real_part.reshape(space, rows, vec_count)
        part[unit, 1] = imag_part.reshape(space, rows, vec_count)

    def ring_copy(unit, step, way):
        out, into, target = (
            (right_out, right_in, right) if way == 0 else (left_out, left_in, left)
        )
        held = pl.ds(way, 1) if step == 1 else pl.ds(0, 2)
        return remote(
            out.at[unit, step - 1, held], into.at[unit, step - 1, held],
            rs_send.at[way, unit, step - 1], rs_recv.at[way, unit, step - 1],
            {"space": target},
        )

    def reduce_step(unit, step):
        for way in range(2):
            into, out = (right_in, right_out) if way == 0 else (left_in, left_out)
            ahead = half - step + 1
            chunk = lax.rem(me + ahead if way == 0 else me + space - ahead, space)
            if step > 1:
                ring_copy(unit, step - 1, way).wait_recv()
            for c in (way,) if step == 1 else (0, 1):
                value = part[unit, c, chunk]
                if step > 2 or (step == 2 and c == way):
                    value = value + into[unit, step - 2, c].astype(F32)
                out[unit, step - 1, c] = value.astype(BF16)
            launch(ring_copy(unit, step, way))

    def reduce_end(unit, m, t):
        for way in range(2):
            if half:
                ring_copy(unit, half, way).wait_recv()
        for c in range(2):
            value = part[unit, c, me]
            if half > 1 or (half and c == 0):
                value = value + right_in[unit, half - 1, c].astype(F32)
            if half > 1 or (half and c == 1):
                value = value + left_in[unit, half - 1, c].astype(F32)
            reduced[m, t, c] = value.astype(BF16)

    def local_time(pair, end):
        return jnp.clip(pairs_ref[pair, end] - group * times, 0, times - 1)

    def chosen_time(m, which):
        return pick(which, [reduced[m, t] for t in range(times)])

    def swap_copy(m, step):
        return remote(
            swap_out.at[m, step], swap_in.at[m, step], swap_send.at[m, step],
            swap_recv.at[m, step], {"tm": lax.rem(group + step, groups)},
        )

    def swap_start(m):
        for step in range(groups):
            owner = lax.rem(group + step, groups)
            for q in range(pair_dev):
                rows_of = chosen_time(m, local_time(owner * pair_dev + q, 1))
                swap_out[m, step, :, q] = rows_of
            if step:
                launch(swap_copy(m, step))

    def gather_copy(m, step, way):
        target = right if way == 0 else left
        chunk = lax.rem(me + space - step + 1 if way == 0 else me + step - 1, space)
        held = pl.ds(way, 1) if step == half else pl.ds(0, 2)
        return remote(
            source.at[m, chunk, held], source.at[m, chunk, held],
            ag_send.at[way, m, step - 1], ag_recv.at[way, m, step - 1],
            {"space": target},
        )

    def gather_start(m):
        for step in range(1, groups):
            swap_copy(m, step).wait_recv()
        for q in range(pair_dev):
            holder = lax.div(pairs_ref[group * pair_dev + q, 1], times)
            back = lax.rem(group + groups - holder, groups)
            held = [swap_out[m, 0, :, q]] + [swap_in[m, s, :, q] for s in range(1, groups)]
            source[m, me, :, q] = pick(back, held)
        for way in range(2):
            if half:
                launch(gather_copy(m, 1, way))

    def gather_step(m, step):
        for way in range(2):
            gather_copy(m, step - 1, way).wait_recv()
            launch(gather_copy(m, step, way))

    def sink_times_mixed(m):
        made = []
        for q in range(pair_dev):
            sink = chosen_time(m, local_time(group * pair_dev + q, 0))
            mixed_re = flat_rows(mixed[:, 0, q])
            mixed_im = flat_rows(mixed[:, 1, q])
            real_part = nn_dot(sink[0], mixed_re) - nn_dot(sink[1], mixed_im)
            imag_part = nn_dot(sink[0], mixed_im) + nn_dot(sink[1], mixed_re)
            made.append((real_part.astype(BF16), imag_part.astype(BF16)))
        return made

    def finish(m, made):
        for way in range(2):
            if half:
                gather_copy(m, half, way).wait_recv()
        for q in range(pair_dev):
            real, imag = made[q]
            source_re = flat_rows(source[m, :, 0, q])
            source_im = flat_rows(source[m, :, 1, q])
            out_ref[q, m, 0] = (nt_dot(real, source_re) + nt_dot(imag, source_im)).astype(BF16)
            out_ref[q, m, 1] = (nt_dot(imag, source_re) - nt_dot(real, source_im)).astype(BF16)

    units = [(m, t) for m in range(moms) for t in range(times)]
    lag = 2
    for unit, (m, t) in enumerate(units):
        build(unit, m, t)
        if half:
            reduce_step(unit, 1)
        if half > 1 and unit >= lag:
            reduce_step(unit - lag, 2)
    for unit in range(max(len(units) - lag, 0), len(units)):
        if half > 1:
            reduce_step(unit, 2)
    for step in range(3, half + 1):
        for unit in range(len(units)):
            reduce_step(unit, step)

    for step in range(1, space):
        mix_hop(step, me).wait_recv()
        launch(core_hop(step))

    made = []
    for unit, (m, t) in enumerate(units):
        reduce_end(unit, m, t)
        if t == times - 1:
            swap_start(m)
            if m == 0:
                for step in range(space):
                    core_hop(step).wait_recv()
            made.append(sink_times_mixed(m))
            if m:
                gather_start(m - 1)
    gather_start(moms - 1)
    for step in range(2, half + 1):
        for m in range(moms):
            gather_step(m, step)
    for m in range(moms):
        finish(m, made[m])
    for copy in sent:
        copy.wait_send()


def local(eigvecs, momenta, pairs, spin_weights, perambulators):
    times, _, colours, vec_count, sites = eigvecs.shape
    pair_dev, _, spin, _, rows, _ = perambulators.shape
    moms = momenta.shape[0]
    space = lax.axis_size("space")
    groups = lax.axis_size("tm")
    half = max(space // 2, 1)
    units = moms * times
    dims = (space, groups, times, moms, colours, vec_count, sites, pair_dev, spin)
    smem = pl.BlockSpec(memory_space=pltpu.SMEM)
    hbm = pl.BlockSpec(memory_space=pl.ANY)
    dma = pltpu.SemaphoreType.DMA
    ring = pltpu.VMEM((units, half, 2, rows, vec_count), BF16)
    swap = pltpu.VMEM((moms, groups, 2, pair_dev, rows, vec_count), BF16)
    return pl.pallas_call(
        functools.partial(kernel, dims),
        out_shape=jax.ShapeDtypeStruct((pair_dev, moms, 2, rows, vec_count), BF16),
        in_specs=[smem, smem, smem, hbm, hbm],
        out_specs=pl.BlockSpec(memory_space=pltpu.VMEM),
        scratch_shapes=[
            pltpu.VMEM((times, vec_count, 2 * colours * sites), BF16),
            pltpu.VMEM((vec_count, 2 * colours * sites), BF16),
            pltpu.VMEM((moms, 2, 8, sites), F32),
            pltpu.VMEM((pair_dev, spin, spin, rows, vec_count), BF16),
            pltpu.VMEM((units, 2, space, rows, vec_count), F32),
            ring, ring, ring, ring,
            pltpu.VMEM((moms, times, 2, rows, vec_count), BF16),
            swap, swap,
            pltpu.VMEM((moms, space, 2, pair_dev, rows, vec_count), BF16),
            pltpu.VMEM((space, 2, pair_dev, rows, vec_count), BF16),
            dma((times, 2, colours)), dma(()),
            dma((2, units, half)), dma((2, units, half)),
            dma((moms, groups)), dma((moms, groups)),
            dma((2, moms, half)), dma((2, moms, half)),
            dma((space,)), dma((space,)), dma((space,)), dma((space,)),
        ],
        compiler_params=pltpu.CompilerParams(collective_id=0, has_side_effects=True),
    )(pairs, spin_weights, momenta, eigvecs, perambulators)


def solution(mesh):
    return jax.shard_map(
        local,
        mesh=mesh,
        in_specs=(
            P(("ens", "tm"), None, None, None, "space"),
            P("mom", None),
            P(),
            P(),
            P(("ens", "tm"), None, None, None, "space", None),
        ),
        out_specs=P(("ens", "tm"), "mom", None, "space", None),
        check_vma=False,
    )
```

time: 120 us -> 42 us (0.35)
  blocking collectives: 93.1 us -> 0 us
  Pallas kernels: 0 us -> 40.2 us
  matrix products: 15.5 us -> 0 us
  starting transfers between devices: 3.89 us -> 0 us
  local copies, waits for them, and re-layouts: 5.32 us -> 1.57 us
  other arithmetic: 1.86 us -> 0 us
    psum x1 -> x0, blocking collectives: 79.3 us -> none  [local(): whole = lax.psum(partial_value, 'space').astype(jnp.bfloat16)]
    pallas_call x0 -> x1, Pallas kernels: none -> 40.2 us  [local(): pl.pallas_call(functools.partial(kernel, dims), out_shape=jax.ShapeDtypeS...]
    dot_general x27 -> x0, matrix products: 15.5 us -> none  [the longest x4 3.57 us: elemental_terms(): lax.dot_general(imag_vec, imag_turned, contract_dims, preferred_element_t...]
    all_gather x1 -> x0, blocking collectives: 13.8 us -> none  [local(): lax.all_gather(mixed_peramb, 'space', axis=2, tiled=True)]
    all_to_all x1 -> x0, starting transfers between devices: 3.89 us -> none  [local(): lax.all_to_all(outgoing, 'tm', split_axis=0, concat_axis=0, tiled=True)]
    convert_element_type x2 -> x0, local copies, waits for them, and re-layouts: 3.68 us -> none  [the longest x1 2.54 us: local(): whole = lax.psum(partial_value, 'space').astype(jnp.bfloat16)]
  transfers between devices with their start and end apart: 1 -> 0, of which waited for: 0 -> 0; matrix products, arithmetic and copies ran while one was open for 3% -> 0% of each run, Pallas kernels for 0% -> 0%
where the time goes in v1:
time: 42 us; the launch traced here: 41.8 us
  Pallas kernels  40.2 us (96%)
  local copies, waits for them, and re-layouts  1.57 us (4%)
    pallas_call x1, Pallas kernels, local(): pl.pallas_call(functools.partial(kernel, dims), out_shape=jax.ShapeDtypeS...  40.2 us
    unnamed x1, local copies, waits for them, and re-layouts  1.57 us

profile of v1, /device:TPU:0, one launch (start us, length us, event | category | flops | bytes accessed | tf_op | source)
XLA Modules:
  0.0 41.8 jit_solution(3830101365013410352)
XLA Ops:
  0.0 40.2 %shard_map.55 = bf16[1,2,2,64,256]{4,3,2,1,0:T(8,128)(2,1)} custom-call(s32[2,2]{1,0:T(2,128)} %pairs_ref.1, f32[4,4]{1,0:T(4,128)} %spin_ref.1, s32[2,3]{1,0:T(2,128)} %mom_ref.1, bf16[2,2,3,256,512]{4,3,2,1,0:T(8,128)(2,1)} %eig_ref.1, bf16[1,2,4,4,64,256]{5,4,3,2,1,0:T(8,128)(2,1)} %per_ref.1), custom_call_target="tpu_custom_call" | custom-call | tf_op jit(solution)/shard_map/pallas_call | solution.py:328
  40.3 1.6 %copy.7 = bf16[1,2,2,64,256]{4,3,2,1,0:T(8,128)(2,1)} copy(bf16[1,2,2,64,256]{4,3,2,1,0:T(8,128)(2,1)} %shard_map.55) | data formatting | bytes 262144

commit v2 on v1

v2 whole, which is shorter than its diff:
```python
import functools
import math

import jax
import jax.numpy as jnp
from jax import lax
from jax.experimental import pallas as pl
from jax.experimental.pallas import tpu as pltpu
from jax.sharding import PartitionSpec as P

LAT = 48
MESH = pl.DeviceIdType.MESH
F32 = jnp.float32
BF16 = jnp.bfloat16
NT = (((1,), (1,)), ((), ()))
ROW_BLOCK = 32


def nt_dot(left, right):
    return lax.dot_general(left, right, NT, preferred_element_type=F32)


def nn_dot(left, right):
    return jnp.dot(left, right, preferred_element_type=F32)


def flat_rows(chunks):
    count, rows, cols = chunks.shape
    if rows % 16:
        return chunks.astype(F32).reshape(count * rows, cols).astype(chunks.dtype)
    return chunks.reshape(count * rows, cols)


def pick(index, values):
    chosen = values[0]
    for which in range(1, len(values)):
        chosen = jnp.where(index == which, values[which], chosen)
    return chosen


def halves(value):
    high = value.astype(BF16)
    return high, (value - high.astype(F32)).astype(BF16)


def kernel(
    dims, pairs_ref, spin_ref, mom_ref, eig_ref, per_ref, out_ref,
    vecs, turned, trig, per_buf, part, right_out, right_in, left_out, left_in,
    total_buf, reduced, swap_out, swap_in, source, mixed,
    eig_sem, per_sem, rs_send, rs_recv, swap_send, swap_recv, ag_send, ag_recv,
    mix_send, mix_recv, core_send, core_recv,
):
    (space, groups, times, moms, colours, vec_count, sites, pair_dev, spin) = dims
    rows = vec_count // space
    last = space - 1
    width = colours * sites
    me = lax.axis_index("space")
    group = lax.axis_index("tm")
    core = lax.axis_index("mom")
    right = lax.rem(me + 1, space)
    left = lax.rem(me + space - 1, space)
    other_core = 1 - core
    sent = []

    barrier = pltpu.get_barrier_semaphore()
    friends = [{"space": lax.rem(me + step, space)} for step in range(1, space)]
    friends += [{"tm": lax.rem(group + step, groups)} for step in range(1, groups)]
    friends += [{"mom": other_core}]
    for friend in friends:
        pl.semaphore_signal(barrier, inc=1, device_id=friend, device_id_type=MESH)

    def remote(src, dst, send_sem, recv_sem, target):
        return pltpu.make_async_remote_copy(
            src_ref=src, dst_ref=dst, send_sem=send_sem, recv_sem=recv_sem,
            device_id=target, device_id_type=MESH,
        )

    def launch(copy):
        copy.start()
        sent.append(copy)

    per_copy = pltpu.make_async_copy(per_ref.at[:, core], per_buf, per_sem)
    per_copy.start()
    eig_copies = []
    for t in range(times):
        of_time = []
        for c in range(2):
            for colour in range(colours):
                first = (c * colours + colour) * sites
                copy = pltpu.make_async_copy(
                    eig_ref.at[t, c, colour], vecs.at[t, :, pl.ds(first, sites)],
                    eig_sem.at[t, c, colour],
                )
                copy.start()
                of_time.append(copy)
        eig_copies.append(of_time)

    site = (lax.broadcasted_iota(jnp.int32, (8, sites), 1) + me * sites).astype(F32)
    line = jnp.floor((site + 0.5) * (1.0 / LAT))
    xcoord = site - line * LAT
    zcoord = jnp.floor((line + 0.5) * (1.0 / LAT))
    ycoord = line - zcoord * LAT
    for m in range(moms):
        turns = (
            mom_ref[m, 0].astype(F32) * xcoord
            + mom_ref[m, 1].astype(F32) * ycoord
            + mom_ref[m, 2].astype(F32) * zcoord
        )
        angle = turns * (2.0 * math.pi / LAT)
        trig[m, 0] = jnp.cos(angle)
        trig[m, 1] = jnp.sin(angle)

    per_copy.wait()
    for q in range(pair_dev):
        total = jnp.zeros((rows, vec_count), F32)
        for a in range(spin):
            for b in range(spin):
                total = total + spin_ref[a, b] * per_buf[q, a, b].astype(F32)
        mixed[me, core, q] = total.astype(BF16)

    pl.semaphore_wait(barrier, len(friends))

    def mix_hop(step, owner):
        return remote(
            mixed.at[owner, core], mixed.at[owner, core], mix_send.at[step - 1],
            mix_recv.at[step - 1], {"space": lax.rem(me + step, space)},
        )

    def core_hop(step):
        owner = lax.rem(me + space - step, space)
        return remote(
            mixed.at[owner, core], mixed.at[owner, core], core_send.at[step],
            core_recv.at[step], {"mom": other_core},
        )

    for step in range(1, space):
        launch(mix_hop(step, me))
    launch(core_hop(0))

    first_time = jnp.clip(pairs_ref[group * pair_dev, 0] - group * times, 0, times - 1)

    def slot_of(pair, end):
        t = jnp.clip(pairs_ref[pair, end] - group * times, 0, times - 1)
        return lax.rem(t - first_time + times, times)

    def build(unit, m, slot):
        if unit == 0:
            for of_time in eig_copies:
                for copy in of_time:
                    copy.wait()
        t = lax.rem(first_time + slot, times)
        cosine = trig[m, 0][None]
        sine = trig[m, 1][None]

        def block(step, carry):
            first = pl.multiple_of(step * ROW_BLOCK, ROW_BLOCK)
            span = pl.ds(first, ROW_BLOCK)
            for colour in range(colours):
                real_at = pl.ds(colour * sites, sites)
                imag_at = pl.ds((colours + colour) * sites, sites)
                shape = (ROW_BLOCK // 8, 8, sites)
                real = vecs[t, span, real_at].astype(F32).reshape(shape)
                imag = vecs[t, span, imag_at].astype(F32).reshape(shape)
                turned[span, real_at] = (
                    (cosine * real + sine * imag).reshape(ROW_BLOCK, sites).astype(BF16)
                )
                turned[span, imag_at] = (
                    (cosine * imag - sine * real).reshape(ROW_BLOCK, sites).astype(BF16)
                )
            return carry

        lax.fori_loop(0, vec_count // ROW_BLOCK, block, 0)
        real_part = nt_dot(vecs[t], turned[...])
        imag_part = nt_dot(vecs[t, :, :width], turned[:, width:]) - nt_dot(
            vecs[t, :, width:], turned[:, :width]
        )
        part[unit, 0] = real_part.reshape(space, rows, vec_count)
        part[unit, 1] = imag_part.reshape(space, rows, vec_count)

    ends_first = sorted(range(space), key=lambda chunk: min(chunk, last - chunk))

    def swap_copy(m, step, chunk):
        return remote(
            swap_out.at[m, step, chunk], swap_in.at[m, step, chunk],
            swap_send.at[m, step, chunk], swap_recv.at[m, step, chunk],
            {"tm": lax.rem(group + step, groups)},
        )

    def swap_start(m):
        for chunk in ends_first:
            for step in range(1, groups):
                owner = lax.rem(group + step, groups)
                for q in range(pair_dev):
                    slot = slot_of(owner * pair_dev + q, 1)
                    for c in range(2):
                        held = [part[m * times + k, c, chunk] for k in range(times)]
                        swap_out[m, step, chunk, q, c] = pick(slot, held).astype(BF16)
                launch(swap_copy(m, step, chunk))

    def term(job, q, c, chunk):
        kind, m = jobs[job]
        pair = group * pair_dev + q
        if kind == "sink":
            if q == 0:
                return part[m * times, c, chunk]
            return pick(slot_of(pair, 0), [part[m * times + k, c, chunk] for k in range(times)])
        own = pick(slot_of(pair, 1), [part[m * times + k, c, chunk] for k in range(times)])
        holder = lax.div(pairs_ref[pair, 1], times)
        back = lax.rem(group + groups - holder, groups)
        held = [own] + [swap_in[m, step, chunk, q, c].astype(F32) for step in range(1, groups)]
        return pick(back, held)

    def await_swap(job, chunk):
        kind, m = jobs[job]
        if kind == "source":
            for step in range(1, groups):
                swap_copy(m, step, chunk).wait_recv()

    def line_copy(job, chunk, way):
        out, into, target = (
            (right_out, right_in, right) if way == 0 else (left_out, left_in, left)
        )
        return remote(
            out.at[job, chunk], into.at[job, chunk], rs_send.at[way, job, chunk],
            rs_recv.at[way, job, chunk], {"space": target},
        )

    def hop(job, chunk, way, at_end):
        out, into = (right_out, right_in) if way == 0 else (left_out, left_in)
        active = me < chunk if way == 0 else me > chunk
        end = me == 0 if way == 0 else me == last

        @pl.when(active & (end if at_end else jnp.logical_not(end)))
        def _():
            await_swap(job, chunk)
            if not at_end:
                line_copy(job, chunk, way).wait_recv()
            for q in range(pair_dev):
                for c in range(2):
                    value = term(job, q, c, chunk)
                    if not at_end:
                        value = value + into[job, chunk, q, c].astype(F32)
                    out[job, chunk, q, c] = value.astype(BF16)
            line_copy(job, chunk, way).start()

    def hops(job, at_end):
        def step(k, carry):
            hop(job, last - k, 0, at_end)
            hop(job, k, 1, at_end)
            return carry

        lax.fori_loop(0, last, step, 0)

    def reduce_end(job):
        await_swap(job, me)
        for q in range(pair_dev):
            for c in range(2):
                total_buf[q, c] = term(job, q, c, me)
        for way in range(2):
            into = right_in if way == 0 else left_in

            @pl.when(me > 0 if way == 0 else me < last)
            def _():
                line_copy(job, me, way).wait_recv()
                total_buf[...] = total_buf[...] + into[job, me].astype(F32)

        kind, m = jobs[job]
        if kind == "sink":
            reduced[m] = total_buf[...].astype(BF16)
        else:
            for c in range(2):
                source[m, me, c] = total_buf[:, c].astype(BF16)

    def gather_copy(m, chunk, way):
        return remote(
            source.at[m, chunk], source.at[m, chunk], ag_send.at[way, m, chunk],
            ag_recv.at[way, m, chunk], {"space": right if way == 0 else left},
        )

    def gather_start(m):
        @pl.when(me < last)
        def _():
            gather_copy(m, me, 0).start()

        @pl.when(me > 0)
        def _():
            gather_copy(m, me, 1).start()

    def gather_pass(m):
        def step(k, carry):
            for way in range(2):
                chunk = me - k if way == 0 else me + k

                @pl.when(chunk >= 0 if way == 0 else chunk <= last)
                def _():
                    gather_copy(m, chunk, way).wait_recv()

                    @pl.when(me < last if way == 0 else me > 0)
                    def _():
                        gather_copy(m, chunk, way).start()

            return carry

        lax.fori_loop(1, space, step, 0)

    def await_sent():
        def step(chunk, carry):
            for way in range(2):
                @pl.when(me < chunk if way == 0 else me > chunk)
                def _():
                    for job in range(len(jobs)):
                        line_copy(job, chunk, way).wait_send()

                held = (chunk <= me) & (me < last) if way == 0 else (chunk >= me) & (me > 0)

                @pl.when(held)
                def _():
                    for m in range(moms):
                        gather_copy(m, chunk, way).wait_send()

            return carry

        lax.fori_loop(0, space, step, 0)
        for copy in sent:
            copy.wait_send()

    def sink_times_mixed(m):
        made = []
        for q in range(pair_dev):
            sink = reduced[m, q]
            mixed_re = flat_rows(mixed[:, 0, q])
            mixed_im = flat_rows(mixed[:, 1, q])
            real_part = nn_dot(sink[0], mixed_re) - nn_dot(sink[1], mixed_im)
            imag_part = nn_dot(sink[0], mixed_im) + nn_dot(sink[1], mixed_re)
            made.append((halves(real_part), halves(imag_part)))
        return made

    def finish(m, made):
        for q in range(pair_dev):
            real, imag = made[q]
            source_re = flat_rows(source[m, :, 0, q])
            source_im = flat_rows(source[m, :, 1, q])

            def times_source(left, right):
                both = nt_dot(jnp.concatenate(left, 0), right)
                return both[:rows] + both[rows:]

            out_ref[q, m, 0] = (
                times_source(real, source_re) + times_source(imag, source_im)
            ).astype(BF16)
            out_ref[q, m, 1] = (
                times_source(imag, source_re) - times_source(real, source_im)
            ).astype(BF16)

    jobs = [("sink", 0)] + [("source", m) for m in range(moms)]
    jobs += [("sink", m) for m in range(1, moms)]
    sink_job = {m: jobs.index(("sink", m)) for m in range(moms)}
    source_job = {m: jobs.index(("source", m)) for m in range(moms)}
    for m in range(moms):
        for slot in range(times):
            build(m * times + slot, m, slot)
            if m == 0 and slot == 0:
                hops(sink_job[0], True)
        swap_start(m)
    hops(source_job[0], True)
    hops(sink_job[0], False)
    for step in range(1, space):
        mix_hop(step, me).wait_recv()
        launch(core_hop(step))
    for m in range(moms):
        if m + 1 < moms:
            hops(source_job[m + 1], True)
        hops(source_job[m], False)
        reduce_end(source_job[m])
        gather_start(m)
        if m + 1 < moms:
            hops(sink_job[m + 1], True)
        if m:
            gather_pass(m - 1)
    for m in range(1, moms):
        hops(sink_job[m], False)
    for step in range(space):
        core_hop(step).wait_recv()
    reduce_end(sink_job[0])
    made = [sink_times_mixed(0)]
    gather_pass(moms - 1)
    finish(0, made[0])
    for m in range(1, moms):
        reduce_end(sink_job[m])
        finish(m, sink_times_mixed(m))
    await_sent()


def local(eigvecs, momenta, pairs, spin_weights, perambulators):
    times, _, colours, vec_count, sites = eigvecs.shape
    pair_dev, _, spin, _, rows, _ = perambulators.shape
    moms = momenta.shape[0]
    space = lax.axis_size("space")
    groups = lax.axis_size("tm")
    jobs = 2 * moms
    dims = (space, groups, times, moms, colours, vec_count, sites, pair_dev, spin)
    smem = pl.BlockSpec(memory_space=pltpu.SMEM)
    hbm = pl.BlockSpec(memory_space=pl.ANY)
    dma = pltpu.SemaphoreType.DMA
    line = pltpu.VMEM((jobs, space, pair_dev, 2, rows, vec_count), BF16)
    swap = pltpu.VMEM((moms, groups, space, pair_dev, 2, rows, vec_count), BF16)
    return pl.pallas_call(
        functools.partial(kernel, dims),
        out_shape=jax.ShapeDtypeStruct((pair_dev, moms, 2, rows, vec_count), BF16),
        in_specs=[smem, smem, smem, hbm, hbm],
        out_specs=pl.BlockSpec(memory_space=pltpu.VMEM),
        scratch_shapes=[
            pltpu.VMEM((times, vec_count, 2 * colours * sites), BF16),
            pltpu.VMEM((vec_count, 2 * colours * sites), BF16),
            pltpu.VMEM((moms, 2, 8, sites), F32),
            pltpu.VMEM((pair_dev, spin, spin, rows, vec_count), BF16),
            pltpu.VMEM((moms * times, 2, space, rows, vec_count), F32),
            line, line, line, line,
            pltpu.VMEM((pair_dev, 2, rows, vec_count), F32),
            pltpu.VMEM((moms, pair_dev, 2, rows, vec_count), BF16),
            swap, swap,
            pltpu.VMEM((moms, space, 2, pair_dev, rows, vec_count), BF16),
            pltpu.VMEM((space, 2, pair_dev, rows, vec_count), BF16),
            dma((times, 2, colours)), dma(()),
            dma((2, jobs, space)), dma((2, jobs, space)),
            dma((moms, groups, space)), dma((moms, groups, space)),
            dma((2, moms, space)), dma((2, moms, space)),
            dma((space,)), dma((space,)), dma((space,)), dma((space,)),
        ],
        compiler_params=pltpu.CompilerParams(collective_id=0, has_side_effects=True),
    )(pairs, spin_weights, momenta, eigvecs, perambulators)


def solution(mesh):
    return jax.shard_map(
        local,
        mesh=mesh,
        in_specs=(
            P(("ens", "tm"), None, None, None, "space"),
            P("mom", None),
            P(),
            P(),
            P(("ens", "tm"), None, None, None, "space", None),
        ),
        out_specs=P(("ens", "tm"), "mom", None, "space", None),
        check_vma=False,
    )
```

time: 42 us -> 57.7 us (1.37)
  Pallas kernels: 40.2 us -> 56 us
    pallas_call x1, Pallas kernels: 40.2 us -> 56 us  [local(): pl.pallas_call(functools.partial(kernel, dims), out_shape=jax.ShapeDtypeS...]
where the time goes in v2:
time: 57.7 us; the launch traced here: 57.6 us
  Pallas kernels  56 us (97%)
  local copies, waits for them, and re-layouts  1.57 us (3%)
    pallas_call x1, Pallas kernels, local(): pl.pallas_call(functools.partial(kernel, dims), out_shape=jax.ShapeDtypeS...  56 us
    unnamed x1, local copies, waits for them, and re-layouts  1.57 us

profile of v2, /device:TPU:0, one launch (start us, length us, event | category | flops | bytes accessed | tf_op | source)
XLA Modules:
  0.0 57.6 jit_solution(4106418412381150708)
XLA Ops:
  0.0 56.0 %shard_map.55 = bf16[1,2,2,64,256]{4,3,2,1,0:T(8,128)(2,1)} custom-call(s32[2,2]{1,0:T(2,128)} %pairs_ref.1, f32[4,4]{1,0:T(4,128)} %spin_ref.1, s32[2,3]{1,0:T(2,128)} %mom_ref.1, bf16[2,2,3,256,512]{4,3,2,1,0:T(8,128)(2,1)} %eig_ref.1, bf16[1,2,4,4,64,256]{5,4,3,2,1,0:T(8,128)(2,1)} %per_ref.1), custom_call_target="tpu_custom_call" | custom-call | tf_op jit(solution)/shard_map/pallas_call | solution.py:407
  56.0 1.6 %copy.7 = bf16[1,2,2,64,256]{4,3,2,1,0:T(8,128)(2,1)} copy(bf16[1,2,2,64,256]{4,3,2,1,0:T(8,128)(2,1)} %shard_map.55) | data formatting | bytes 262144
